TPU v7x, 32 devices: a whole 2x2x4 slice. The times are simulated.
32 devices in a mesh: dp: 4 (over x, core), space: 8 (over z, y).
Axes of the slice: x: 2, y: 2, z: 4, core: 2. Of those that a mesh axis runs over, the one named last changes fastest.
Arguments:
- section_three: bfloat16 [4, 64, 128, 512], P('dp', 'space'), parts along dimension 0, may hold values from -6 to 6
- section_four: bfloat16 [4, 32, 64, 1024], P('dp', 'space'), parts along dimension 0, may hold values from -6 to 6
- section_five: bfloat16 [4, 16, 32, 2048], P('dp', 'space'), parts along dimension 0, may hold values from -6 to 6
- lateral_three: bfloat16 [512, 256], P('space'), may hold values from -0.25 to 0.25
- lateral_four: bfloat16 [1024, 256], P('space'), may hold values from -0.1875 to 0.1875
- lateral_five: bfloat16 [2048, 256], P('space'), may hold values from -0.125 to 0.125
- lateral_bias_three: float32 [256], replicated, may hold values from -3 to 3
- lateral_bias_four: float32 [256], replicated, may hold values from -3 to 3
- lateral_bias_five: float32 [256], replicated, may hold values from -3 to 3
- output_three: bfloat16 [3, 3, 256, 256], P(None, None, 'space'), may hold values from -0.125 to 0.125
- output_four: bfloat16 [3, 3, 256, 256], P(None, None, 'space'), may hold values from -0.125 to 0.125
- output_five: bfloat16 [3, 3, 256, 256], P(None, None, 'space'), may hold values from -0.125 to 0.125
- output_bias_three: float32 [256], replicated, may hold values from -3 to 3
- output_bias_four: float32 [256], replicated, may hold values from -3 to 3
- output_bias_five: float32 [256], replicated, may hold values from -3 to 3
Outputs:
- level_three: bfloat16 [4, 64, 128, 256], P('dp', 'space'), parts along dimension 0
- level_four: bfloat16 [4, 32, 64, 256], P('dp', 'space'), parts along dimension 0
- level_five: bfloat16 [4, 16, 32, 256], P('dp'), parts along dimension 0
- level_six: bfloat16 [4, 8, 16, 256], P('dp'), parts along dimension 0
There are 4 independent parts, one for each index of `dp`. A program takes and returns all parts, laid end to end along the dimension named above; an argument that names none is the same for every part. Nothing has to cross between parts.
All inputs are finite; a program needn't handle non-finite values.
Results may differ from a plain program's by a relative error of at most 0.0095.
Values may be sent and summed in bfloat16 or wider, within the bound.
A program may use at most 64 MiB of HBM per device.

v0:
```python
import functools

import jax
import jax.numpy as jnp
from jax import lax
from jax.experimental import pallas as pl
from jax.experimental.pallas import tpu as pltpu
from jax.sharding import PartitionSpec as P

F32, BF16 = jnp.float32, jnp.bfloat16


def ring_place(s, n):
    return s // 2 + (s % 2) * (n - 1 - 2 * (s // 2))


def ring_owner(place, n):
    r = (place + 2 * n) % n
    back = r // (n // 2)
    return (1 - back) * (2 * r) + back * (2 * (n - 1 - r) + 1)


def spread(coarse):
    pixels = coarse.shape[0]
    fine = lax.broadcasted_iota(jnp.int32, (2 * pixels, pixels), 0) // 2
    pick = (fine == lax.broadcasted_iota(jnp.int32, (2 * pixels, pixels), 1)).astype(BF16)
    return jnp.dot(pick, coarse, preferred_element_type=F32)


def conv_tile(frame, weight, bias, start, pixels, width):
    rows = jnp.concatenate(
        [frame[pl.ds(pl.multiple_of(start + a * width, 16), pixels), :] for a in range(3)], axis=1
    )
    depth = weight.shape[2]
    part = [
        jnp.dot(
            rows,
            weight[:, c].reshape(3 * depth, weight.shape[3]),
            preferred_element_type=F32,
        )
        for c in range(3)
    ]
    column = lax.broadcasted_iota(jnp.int32, (pixels, 1), 0) % width
    left = jnp.where(column == 0, 0.0, pltpu.roll(part[0], 1, 0))
    right = jnp.where(column == width - 1, 0.0, pltpu.roll(part[2], pixels - 1, 0))
    return part[1] + left + right + bias[...]


def kernel(
    n, dims,
    s3, s4, s5, l3, l4, l5, hb3, hb4, hb5, o3, o4, o5, hc3, hc4, hc5,
    y3, y4, y5, y6,
    v3, v4, v5, w_l5, w_l4, w_l3, w_o3, w_o5, w_o4,
    m3, m4, m5, r3, r4, r5, r6, lb3, lb4, lb5, ob3, ob4, ob5,
    ring_send, ring_recv, core_send, core_recv, map_send, map_recv, halo_send, halo_recv, local_sem,
):
    (rows3, wid3), (rows4, wid4), (rows5, wid5) = dims
    dp, s = lax.axis_index("dp"), lax.axis_index("space")
    core = dp % 2
    partner = (dp + 1 - 2 * core, s)
    place = ring_place(s, n)
    sign = 1 - 2 * core
    hops = (n // 2, n - 1 - n // 2)
    turn = (sign, -sign)
    target = [(dp, ring_owner(place + turn[k], n)) for k in range(2)]
    above, below = (dp, (s + n - 1) % n), (dp, (s + 1) % n)

    full = (w_l5, w_l4, w_l3, w_o3, w_o5, w_o4)
    mine = (l5, l4, l3, o3, o5, o4)
    half = w_l5.shape[1] // 2

    def map_rows(owner):
        size = rows5 * wid5
        return m5.at[pl.ds(pl.multiple_of(wid5 + owner * size, 16), size), :]

    def chunk(a, owner, side):
        cols = pl.ds(pl.multiple_of(side * half, half), half)
        if a < 3:
            size = mine[a].shape[0]
            return full[a].at[pl.ds(pl.multiple_of(owner * size, size), size), cols]
        size = mine[a].shape[2]
        return full[a].at[:, :, pl.ds(pl.multiple_of(owner * size, size), size), cols]

    def own_part(a):
        cols = pl.ds(pl.multiple_of(core * half, half), half)
        return mine[a].at[:, cols] if a < 3 else mine[a].at[:, :, :, cols]

    def own_whole(a):
        if a < 3:
            size = mine[a].shape[0]
            return full[a].at[pl.ds(pl.multiple_of(s * size, size), size), :]
        size = mine[a].shape[2]
        return full[a].at[:, :, pl.ds(pl.multiple_of(s * size, size), size), :]

    local = [pltpu.make_async_copy(mine[a], own_whole(a), local_sem.at[a]) for a in range(6)]
    features = [
        pltpu.make_async_copy(src, dst, local_sem.at[6 + k])
        for k, (src, dst) in enumerate(((s5, v5), (s4, v4), (s3, v3)))
    ]
    biases = [
        pltpu.make_async_copy(src, dst, local_sem.at[13 + k])
        for k, (src, dst) in enumerate(
            ((hb3, lb3), (hb4, lb4), (hb5, lb5), (hc3, ob3), (hc4, ob4), (hc5, ob5))
        )
    ]
    for copy in features + local + biases:
        copy.start()

    barrier = pltpu.get_barrier_semaphore()
    peers = [(dp, (s + d) % n) for d in range(1, n)]
    for device in (*peers, partner):
        pl.semaphore_signal(
            barrier, inc=1, device_id=device, device_id_type=pl.DeviceIdType.MESH
        )
    pl.semaphore_wait(barrier, n)

    def remote(src, dst, send, recv, device):
        return pltpu.make_async_remote_copy(
            src_ref=src, dst_ref=dst, send_sem=send, recv_sem=recv,
            device_id=device, device_id_type=pl.DeviceIdType.MESH,
        )

    sent = []

    def push(a, k, step):
        if step > hops[k]:
            return
        owner = ring_owner(place - turn[k] * (step - 1), n)
        dst = chunk(a, owner, core)
        src = own_part(a) if step == 1 else dst
        copy = remote(src, dst, ring_send.at[a, k, step - 1], ring_recv.at[a, k, step - 1], target[k])
        copy.start()
        sent.append(copy)

    def cross(a, k, step, side, turns):
        owner = ring_owner(place - turns[k] * step, n)
        spot = chunk(a, owner, side)
        j = k * hops[0] + step - 1
        return remote(spot, spot, core_send.at[a, j], core_recv.at[a, j], partner)

    def pull(a, step):
        for k in range(2):
            if step > hops[k]:
                continue
            owner = ring_owner(place - turn[k] * step, n)
            spot = chunk(a, owner, core)
            remote(
                spot, spot, ring_send.at[a, k, step - 1], ring_recv.at[a, k, step - 1], target[k]
            ).wait_recv()
            push(a, k, step + 1)
            copy = cross(a, k, step, core, turn)
            copy.start()
            sent.append(copy)

    def settle(a):
        for k in range(2):
            for step in range(1, hops[k] + 1):
                cross(a, k, step, 1 - core, (turn[1], turn[0])).wait_recv()
        local[a].wait()

    for a in (0, 1, 2):
        push(a, 0, 1)
        push(a, 1, 1)
    waiting = [3, 4, 5]
    for step in range(1, hops[0] + 1):
        if waiting and step > 1:
            a = waiting.pop(0)
            push(a, 0, 1)
            push(a, 1, 1)
        for a in (0, 1, 2):
            pull(a, step)
    while waiting:
        a = waiting.pop(0)
        push(a, 0, 1)
        push(a, 1, 1)
    for a in (3, 4, 5):
        pull(a, 1)

    settle(0)
    features[0].wait()
    for copy in biases:
        copy.wait()
    zero5 = jnp.zeros((wid5, m5.shape[1]), BF16)
    m5[pl.ds(0, wid5), :] = zero5
    m5[pl.ds(m5.shape[0] - wid5, wid5), :] = zero5
    here = pl.multiple_of(wid5 + s * (rows5 * wid5), 16)
    m5[pl.ds(here, rows5 * wid5), :] = (
        jnp.dot(v5[...], w_l5[...], preferred_element_type=F32) + lb5[...]
    ).astype(BF16)
    settle(1)
    features[1].wait()
    for d in range(1, n):
        copy = remote(map_rows(s), map_rows(s), map_send.at[d - 1], map_recv.at[d - 1], peers[d - 1])
        copy.start()
        sent.append(copy)
    for r in range(rows5):
        up = spread(m5[pl.ds(pl.multiple_of(here + r * wid5, 16), wid5), :])
        base = 2 * r * wid4
        lat = jnp.dot(v4[base : base + 2 * wid4, :], w_l4[...], preferred_element_type=F32)
        m4[wid4 + base : wid4 + base + 2 * wid4, :] = (
            lat + lb4[...] + jnp.concatenate([up, up], axis=0)
        ).astype(BF16)
    settle(2)
    features[2].wait()

    def coarse_row(r, carry):
        up = spread(m4[pl.ds(pl.multiple_of(wid4 + r * wid4, 16), wid4), :])
        base = pl.multiple_of(2 * r * wid3, 16)
        lat = jnp.dot(v3[pl.ds(base, 2 * wid3), :], w_l3[...], preferred_element_type=F32)
        m3[pl.ds(pl.multiple_of(wid3 + base, 16), 2 * wid3), :] = (
            lat + lb3[...] + jnp.concatenate([up, up], axis=0)
        ).astype(BF16)
        return carry

    lax.fori_loop(0, rows4 // 2, coarse_row, 0)
    for a in (3, 4, 5):
        pull(a, 2)
    lax.fori_loop(rows4 // 2, rows4, coarse_row, 0)

    halos = []
    for k, (frame, rows, wid) in enumerate(((m4, rows4, wid4), (m3, rows3, wid3))):
        first, last = frame.at[pl.ds(wid, wid), :], frame.at[pl.ds(rows * wid, wid), :]
        top, bottom = frame.at[pl.ds(0, wid), :], frame.at[pl.ds((rows + 1) * wid, wid), :]
        halos.append((
            remote(last, top, halo_send.at[2 * k], halo_recv.at[2 * k], below),
            remote(first, bottom, halo_send.at[2 * k + 1], halo_recv.at[2 * k + 1], above),
        ))

    def start_halos():
        @pl.when(s < n - 1)
        def _():
            for pair in halos:
                pair[0].start()

        @pl.when(s > 0)
        def _():
            for pair in halos:
                pair[1].start()

    for step in range(3, hops[0]):
        for a in (3, 4, 5):
            pull(a, step)
            if step == 3 and a == 3:
                start_halos()
    pull(3, hops[0])

    @pl.when(s > 0)
    def _():
        for pair in halos:
            pair[0].wait_recv()
            pair[1].wait_send()

    @pl.when(s < n - 1)
    def _():
        for pair in halos:
            pair[1].wait_recv()
            pair[0].wait_send()

    for frame, rows, wid in ((m4, rows4, wid4), (m3, rows3, wid3)):
        zero = jnp.zeros((wid, frame.shape[1]), BF16)

        @pl.when(s == 0)
        def _():
            frame[pl.ds(0, wid), :] = zero

        @pl.when(s == n - 1)
        def _():
            frame[pl.ds((rows + 1) * wid, wid), :] = zero

    settle(3)

    def conv(frame, weight, bias, out, rows, wid, tall):
        def tile(i, carry):
            start = pl.multiple_of(i * (tall * wid), 16)
            out[pl.ds(start, tall * wid), :] = conv_tile(
                frame, weight, bias, start, tall * wid, wid
            ).astype(BF16)
            return carry

        lax.fori_loop(0, rows // tall, tile, 0)

    conv(m3, w_o3, ob3, r3, rows3, wid3, 4)
    out3 = pltpu.make_async_copy(r3, y3, local_sem.at[9])
    out3.start()

    pull(4, hops[0])
    pull(5, hops[0])
    settle(4)
    for d in range(1, n):
        spot = map_rows((s + n - d) % n)
        remote(spot, spot, map_send.at[d - 1], map_recv.at[d - 1], peers[d - 1]).wait_recv()
    conv(m5, w_o5, ob5, r5, n * rows5, wid5, 16)
    out5 = pltpu.make_async_copy(r5, y5, local_sem.at[10])
    out5.start()
    take = lax.broadcasted_iota(jnp.int32, (wid5 // 2, wid5), 0) * 2
    pick = (take == lax.broadcasted_iota(jnp.int32, (wid5 // 2, wid5), 1)).astype(BF16)

    def even_row(i, carry):
        row = r5[pl.ds(pl.multiple_of(2 * i * wid5, 16), wid5), :]
        r6[pl.ds(pl.multiple_of(i * (wid5 // 2), 16), wid5 // 2), :] = jnp.dot(
            pick, row, preferred_element_type=F32
        ).astype(BF16)
        return carry

    lax.fori_loop(0, n * rows5 // 2, even_row, 0)
    out6 = pltpu.make_async_copy(r6, y6, local_sem.at[11])
    out6.start()

    settle(5)
    conv(m4, w_o4, ob4, r4, rows4, wid4, rows4)
    out4 = pltpu.make_async_copy(r4, y4, local_sem.at[12])
    out4.start()

    for copy in sent:
        copy.wait_send()
    for copy in (out3, out5, out6, out4):
        copy.wait()


def on_device(n, *arrays):
    s3, s4, s5, l3, l4, l5, lb3, lb4, lb5, o3, o4, o5, ob3, ob4, ob5 = arrays
    dims = tuple(x.shape[1:3] for x in (s3, s4, s5))
    fd = l3.shape[1]
    (rows3, wid3), (rows4, wid4), (rows5, wid5) = dims
    flat = [x.reshape(-1, x.shape[3]) for x in (s3, s4, s5)]
    biases = [b.reshape(1, fd) for b in (lb3, lb4, lb5, ob3, ob4, ob5)]
    anywhere = pl.BlockSpec(memory_space=pl.ANY)
    far = max(n // 2, 1)

    def array(*shape):
        return pltpu.VMEM(shape, BF16)

    def result(pixels):
        return jax.ShapeDtypeStruct((pixels, fd), BF16)

    dma = pltpu.SemaphoreType.DMA
    y3, y4, y5, y6 = pl.pallas_call(
        functools.partial(kernel, n, dims),
        out_shape=(
            result(rows3 * wid3),
            result(rows4 * wid4),
            result(n * rows5 * wid5),
            result(n * rows5 * wid5 // 4),
        ),
        in_specs=[anywhere] * 15,
        out_specs=(anywhere,) * 4,
        scratch_shapes=[
            *(array(*x.shape) for x in flat),
            array(n * l5.shape[0], fd),
            array(n * l4.shape[0], fd),
            array(n * l3.shape[0], fd),
            *(array(3, 3, n * x.shape[2], fd) for x in (o3, o5, o4)),
            array((rows3 + 2) * wid3, fd),
            array((rows4 + 2) * wid4, fd),
            array((n * rows5 + 2) * wid5, fd),
            array(rows3 * wid3, fd),
            array(rows4 * wid4, fd),
            array(n * rows5 * wid5, fd),
            array(n * rows5 * wid5 // 4, fd),
            *(pltpu.VMEM((1, fd), F32) for _ in range(6)),
            dma((6, 2, far)),
            dma((6, 2, far)),
            dma((6, n - 1)),
            dma((6, n - 1)),
            dma((n - 1,)),
            dma((n - 1,)),
            dma((4,)),
            dma((4,)),
            dma((19,)),
        ],
        compiler_params=pltpu.CompilerParams(
            collective_id=0, has_side_effects=True, vmem_limit_bytes=60 * 1024 * 1024
        ),
    )(*flat, l3, l4, l5, *biases[:3], o3, o4, o5, *biases[3:])
    return (
        y3.reshape(1, rows3, wid3, fd),
        y4.reshape(1, rows4, wid4, fd),
        y5.reshape(1, n * rows5, wid5, fd),
        y6.reshape(1, n * rows5 // 2, wid5 // 2, fd),
    )


def solution(mesh):
    split, rows = P("dp", "space", None, None), P("space", None)
    taps = P(None, None, "space", None)
    whole = P("dp", None, None, None)
    return jax.shard_map(
        functools.partial(on_device, mesh.shape["space"]),
        mesh=mesh,
        in_specs=(split,) * 3 + (rows,) * 3 + (P(),) * 3 + (taps,) * 3 + (P(),) * 3,
        out_specs=(split, split, whole, whole),
        check_vma=False,
    )
```

profile of v0, /device:TPU:15, one launch (start us, length us, event | category | flops | bytes accessed | tf_op | source)
XLA Modules:
  0.0 52.1 jit_solution(2948003459830567740)
XLA Ops:
  0.6 47.1 %shard_map.174 = (bf16[1024,256]{1,0:T(8,128)(2,1)}, bf16[256,256]{1,0:T(8,128)(2,1)}, bf16[512,256]{1,0:T(8,128)(2,1)}, bf16[128,256]{1,0:T(8,128)(2,1)}) custom-call(bf16[1024,512]{1,0:T(8,128)(2,1)} %bitcast.13, bf16[256,1024]{1,0:T(8,128)(2,1)} %bitcast.15, bf16[64,2048]{1,0:T(8,128)(2,1)} %bitcast.17, bf16[64,256]{1,0:T(8,128)(2,1)} %l3.1, ...), custom_call_target="tpu_custom_call" | custom-call | tf_op jit(solution)/shard_map/pallas_call | solution.py:337
  47.7 0.0 copy-start.1
  47.7 1.9 %copy.23 = bf16[1,8,128,256]{3,2,1,0:T(8,128)(2,1)} copy(bf16[1,8,128,256]{3,2,1,0:T(8,128)(2,1)} %bitcast.14) | data formatting | bytes 1048576
  49.6 0.0 copy-done.1
  49.6 0.0 copy-start
  49.6 0.7 %copy.24 = bf16[1,4,64,256]{3,2,1,0:T(8,128)(2,1)} copy(bf16[1,4,64,256]{3,2,1,0:T(8,128)(2,1)S(1)} %bitcast.18) | data formatting | bytes 262144
  50.3 0.3 copy-done
  50.6 0.0 copy-start.2
  50.6 0.7 %copy.25 = bf16[1,16,32,256]{3,2,1,0:T(8,128)(2,1)} copy(bf16[1,16,32,256]{3,2,1,0:T(8,128)(2,1)S(1)} %bitcast.16) | data formatting | bytes 524288
  51.3 0.2 copy-done.2
  51.5 0.6 %copy.26 = bf16[1,8,16,256]{3,2,1,0:T(8,128)(2,1)} copy(bf16[1,8,16,256]{3,2,1,0:T(8,128)(2,1)S(1)} %bitcast.19) | data formatting | bytes 131072
Async XLA Ops:
  47.7 1.9 %copy-start.1 = (bf16[256,256]{1,0:T(8,128)(2,1)S(1)}, bf16[256,256]{1,0:T(8,128)(2,1)}, u32[]{:S(2)}) copy-start(bf16[256,256]{1,0:T(8,128)(2,1)} %get-tuple-element.9) | copy-start | bytes 393220
  49.6 1.0 %copy-start = (bf16[512,256]{1,0:T(8,128)(2,1)S(1)}, bf16[512,256]{1,0:T(8,128)(2,1)}, u32[]{:S(2)}) copy-start(bf16[512,256]{1,0:T(8,128)(2,1)} %get-tuple-element.10) | copy-start | bytes 786436
  50.6 0.9 %copy-start.2 = (bf16[128,256]{1,0:T(8,128)(2,1)S(1)}, bf16[128,256]{1,0:T(8,128)(2,1)}, u32[]{:S(2)}) copy-start(bf16[128,256]{1,0:T(8,128)(2,1)} %get-tuple-element.11) | copy-start | bytes 196612
where the time goes:
time: 52.3 us; the launch traced here: 52.1 us
  Pallas kernels  47.1 us (90%)
  local copies, waits for them, and re-layouts  4.4 us (8%)
  between operations  0.66 us (1%)
    pallas_call x1, Pallas kernels, on_device(): pl.pallas_call(functools.partial(kernel, n, dims), out_shape=(result(rows...  47.1 us
    unnamed x10, local copies, waits for them, and re-layouts  4.4 us

commit v1 on v0

v1 whole, which is shorter than its diff:
```python
import functools

import jax
import jax.numpy as jnp
from jax import lax
from jax.experimental import pallas as pl
from jax.experimental.pallas import tpu as pltpu
from jax.sharding import PartitionSpec as P

F32, BF16 = jnp.float32, jnp.bfloat16
L5, L4, L3, O3, O5, O4 = range(6)


def ring_place(s, n):
    return s // 2 + (s % 2) * (n - 1 - 2 * (s // 2))


def ring_owner(place, n):
    r = (place + 2 * n) % n
    back = r // (n // 2)
    return (1 - back) * (2 * r) + back * (2 * (n - 1 - r) + 1)


def spread(coarse):
    pixels = coarse.shape[0]
    fine = lax.broadcasted_iota(jnp.int32, (2 * pixels, pixels), 0) // 2
    pick = (fine == lax.broadcasted_iota(jnp.int32, (2 * pixels, pixels), 1)).astype(BF16)
    return jnp.dot(pick, coarse, preferred_element_type=F32)


def conv_tile(frame, weight, bias, start, pixels, width):
    rows = jnp.concatenate(
        [frame[pl.ds(pl.multiple_of(start + a * width, 16), pixels), :] for a in range(3)], axis=1
    )
    depth = weight.shape[2]
    part = [
        jnp.dot(
            rows,
            weight[:, c].reshape(3 * depth, weight.shape[3]),
            preferred_element_type=F32,
        )
        for c in range(3)
    ]
    column = lax.broadcasted_iota(jnp.int32, (pixels, 1), 0) % width
    left = jnp.where(column == 0, 0.0, pltpu.roll(part[0], 1, 0))
    right = jnp.where(column == width - 1, 0.0, pltpu.roll(part[2], pixels - 1, 0))
    return part[1] + left + right + bias[...]


def conv(frame, weight, bias, out, rows, wid, tall, first=0):
    def tile(i, carry):
        start = pl.multiple_of(i * (tall * wid), 16)
        out[pl.ds(start, tall * wid), :] = conv_tile(
            frame, weight, bias, start, tall * wid, wid
        ).astype(BF16)
        return carry

    lax.fori_loop(first, rows // tall, tile, 0)


def shared(unit, parts, split):
    if not split:
        return 0
    return parts // 2 // unit * unit if unit > 1 else parts // 3


def schedule(hops, lent, halved, line):
    begin = (2.34, 0.36, 2.39, 5.66, 3.55, 2.90)
    pace = (2.10, 2.62, 2.56, 3.93, 4.11, 5.31)
    lag = (2.50, 4.29, 5.09, 6.74, 3.76, 6.04)
    settled, half_to_five, line_lag, three_to_conv, five_lag, swap = 1.21, 4.39, 6.36, 20.56, 16.95, 3.70
    events = []
    ready = []
    for a in range(6):
        events.append((begin[a], "push", a, 0, 0))
        for k in range(2):
            for step in range(1, hops[k] + 1):
                at = begin[a] + pace[a] * step
                events.append((at, "pull", a, k, step))
                if lent[a]:
                    events.append((at + lag[a], "mate", a, k, step))
        ready.append(begin[a] + pace[a] * hops[0] + (lag[a] if lent[a] else 0.0) + 0.001)
    five = ready[L5] + settled
    if halved:
        events += [(swap, "swap", 0, 0, 0), (five, "half", 5, 0, 0)]
        five += half_to_five
    four = max(five, ready[L4] + settled) + 0.01
    three = max(four, ready[L3] + settled) + 0.01
    events += [(five, "merge", 5, 0, 0), (four, "merge", 4, 0, 0), (three, "merge", 3, 0, 0)]
    events += [(five + line_lag + 0.01 * j, "line", j, 0, 0) for j in range(1, line)]
    late = max(three + three_to_conv, ready[O3])
    events.append((late, "conv", 3, 0, 0))
    events.append((max(late + 0.01, five + line_lag + 0.5, ready[O5] + five_lag), "conv", 5, 0, 0))
    return [e[1:] for e in sorted(events, key=lambda e: e[0])]


def kernel(
    n, dims, dps,
    s3, s4, s5, l3, l4, l5, hb3, hb4, hb5, o3, o4, o5, hc3, hc4, hc5,
    r3, r5, r6, m4, w_o4, ob4,
    v3, v4, v5, v5_mate, own5, out5, in5, w_l5, w_l4, w_l3, w_o3, w_o5,
    m3, m5, lb3, lb4, lb5, ob3, ob5,
    ring_send, ring_recv, mate_send, mate_recv, core_send, core_recv,
    line_send, line_recv, pair_send, pair_recv, swap_send, swap_recv,
    halo_send, halo_recv, load5_sem, local_sem,
):
    (rows3, wid3), (rows4, wid4), (rows5, wid5) = dims
    dp, s = lax.axis_index("dp"), lax.axis_index("space")
    core = dp % 2
    plane = (dp // 2) % 2
    partner = (dp + 1 - 2 * core, s)
    mate = (dp + 2 - 4 * plane, s)
    paired = dps % 4 == 0
    place = ring_place(s, n)
    sign = 1 - 2 * core
    hops = (n // 2, n - 1 - n // 2)
    turn = (sign, -sign)
    target = [(dp, ring_owner(place + turn[k], n)) for k in range(2)]
    above, below = (dp, (s + n - 1) % n), (dp, (s + 1) % n)

    full = (w_l5, w_l4, w_l3, w_o3, w_o5, w_o4)
    mine = (l5, l4, l3, o3, o5, o4)
    half = w_l5.shape[1] // 2

    barrier = pltpu.get_barrier_semaphore()
    friends = [*target, partner] + ([mate] if paired else [])
    for device in friends:
        pl.semaphore_signal(
            barrier, inc=1, device_id=device, device_id_type=pl.DeviceIdType.MESH
        )

    parts = [mine[a].shape[0] for a in range(3)] + [3] * 3
    lent = [shared(16 if a < 3 else 1, parts[a], paired) for a in range(6)]
    halved = v5.shape[0] == 2
    if halved:
        parts[L5], lent[L5] = parts[L5] // 2, 0

    def chunk(a, owner, side, first, count):
        cols = pl.ds(pl.multiple_of(side * half, half), half)
        if a < 3:
            return full[a].at[pl.ds(pl.multiple_of(owner * parts[a] + first, 16), count), cols]
        size = mine[a].shape[2]
        return full[a].at[
            pl.ds(first, count), :, pl.ds(pl.multiple_of(owner * size, size), size), cols
        ]

    def ring_part(a, owner):
        return chunk(a, owner, core, plane * lent[a], parts[a] - lent[a])

    def mate_part(a, owner, sender):
        return chunk(a, owner, core, sender * (parts[a] - lent[a]), lent[a])

    def own_whole(a):
        if a < 3:
            size = parts[a]
            return full[a].at[pl.ds(pl.multiple_of(s * size, size), size), :]
        size = mine[a].shape[2]
        return full[a].at[:, :, pl.ds(pl.multiple_of(s * size, size), size), :]

    def own_shard(a):
        if a == L5 and halved:
            return mine[a].at[pl.ds(pl.multiple_of(plane * parts[a], 16), parts[a]), :]
        return mine[a]

    def bulk(a, count, side):
        cols = pl.ds(pl.multiple_of(side * half, half), half)
        if a < 3:
            return full[a].at[pl.ds(0, (n - 1) * count), cols]
        return full[a].at[pl.ds(0, count), :, pl.ds(0, (n - 1) * mine[a].shape[2]), cols]

    local = [pltpu.make_async_copy(own_shard(a), own_whole(a), local_sem.at[a]) for a in range(6)]
    features = [
        pltpu.make_async_copy(src, dst, local_sem.at[6 + k])
        for k, (src, dst) in enumerate(((s4, v4), (s3, v3)))
    ]
    biases = [
        pltpu.make_async_copy(src, dst, local_sem.at[8 + k])
        for k, (src, dst) in enumerate(
            ((hb3, lb3), (hb4, lb4), (hb5, lb5), (hc3, ob3), (hc4, ob4), (hc5, ob5))
        )
    ]
    pieces = v5.shape[0]
    load5 = [
        pltpu.make_async_copy(s5.at[:, pl.ds(0, v5.shape[2])], v5.at[q], load5_sem.at[q])
        for q in range(pieces)
    ]
    for copy in local:
        copy.start()
    if halved:
        for q in range(2):
            for owner in range(n):
                pltpu.make_async_copy(
                    s5.at[:, pl.ds((2 * owner + q) * parts[L5], parts[L5])],
                    v5.at[q, :, pl.ds(owner * parts[L5], parts[L5])],
                    load5_sem.at[q],
                ).start()
    else:
        load5[0].start()
    for copy in features + biases:
        copy.start()

    zero5 = jnp.zeros((wid5, m5.shape[1]), BF16)
    m5[pl.ds(0, wid5), :] = zero5
    m5[pl.ds(m5.shape[0] - wid5, wid5), :] = zero5
    with jax.named_scope("meet"):
        pl.semaphore_wait(barrier, len(friends))

    def remote(src, dst, send, recv, device):
        return pltpu.make_async_remote_copy(
            src_ref=src, dst_ref=dst, send_sem=send, recv_sem=recv,
            device_id=device, device_id_type=pl.DeviceIdType.MESH,
        )

    def send(a, k, step, owner):
        if step <= hops[k]:
            spot = ring_part(a, owner)
            remote(spot, spot, ring_send.at[a], ring_recv.at[a, k, step - 1], target[k]).start()

    def cross(a, spot):
        remote(spot, spot, core_send.at[a], core_recv.at[a], partner).start()

    def push(a):
        local[a].wait()
        for k in range(2):
            send(a, k, 1, s)

    def pull(a, k, step):
        owner = ring_owner(place - turn[k] * step, n)
        spot = ring_part(a, owner)
        remote(spot, spot, ring_send.at[a], ring_recv.at[a, k, step - 1], target[k]).wait_recv()
        send(a, k, step + 1, owner)
        if lent[a]:
            gift = mate_part(a, owner, plane)
            remote(gift, gift, mate_send.at[a], mate_recv.at[a, k, step - 1], mate).start()
        cross(a, spot)

    def accept(a, k, step):
        owner = ring_owner(place - turn[k] * step, n)
        spot = mate_part(a, owner, 1 - plane)
        remote(spot, spot, mate_send.at[a], mate_recv.at[a, k, step - 1], mate).wait_recv()
        cross(a, spot)

    def settle(a):
        spot = bulk(a, parts[a], 1 - core)
        remote(spot, spot, core_send.at[a], core_recv.at[a], partner).wait_recv()

    def map_rows(owner):
        size = rows5 * wid5
        return m5.at[pl.ds(pl.multiple_of(wid5 + owner * size, 16), size), :]

    across = s + 1 - 2 * (s % 2)

    def line_copy(j, owner):
        spot = map_rows(owner)
        peer = (dp, (s + 2 * j) % n)
        return remote(spot, spot, line_send.at[j - 1], line_recv.at[j - 1], peer)

    def pair_copy(j, owner):
        spot = map_rows(owner)
        return remote(spot, spot, pair_send.at[j], pair_recv.at[j], (dp, across))

    def line_pull(j):
        owner = (s + n - 2 * j) % n
        line_copy(j, owner).wait_recv()
        pair_copy(j, owner).start()

    if halved:
        swap = remote(v5.at[1 - plane], v5_mate, swap_send.at[0], swap_recv.at[0], mate)
        partial = remote(out5, in5, swap_send.at[1], swap_recv.at[1], mate)

    def half_five():
        settle(L5)
        swap.wait_recv()
        rows = jnp.concatenate([v5[plane], v5_mate[...]], axis=0)
        sums = jnp.dot(rows, w_l5[...], preferred_element_type=F32)
        own5[...] = sums[: own5.shape[0]]
        out5[...] = sums[own5.shape[0] :]
        partial.start()

    here = pl.multiple_of(wid5 + s * (rows5 * wid5), 16)
    halos = []
    for k, (frame, rows, wid) in enumerate(((m4, rows4, wid4), (m3, rows3, wid3))):
        first, last = frame.at[pl.ds(wid, wid), :], frame.at[pl.ds(rows * wid, wid), :]
        top, bottom = frame.at[pl.ds(0, wid), :], frame.at[pl.ds((rows + 1) * wid, wid), :]
        halos.append((
            remote(last, top, halo_send.at[2 * k], halo_recv.at[2 * k], below),
            remote(first, bottom, halo_send.at[2 * k + 1], halo_recv.at[2 * k + 1], above),
        ))

    def start_halo(pair):
        @pl.when(s < n - 1)
        def _():
            pair[0].start()

        @pl.when(s > 0)
        def _():
            pair[1].start()

    def end_halo(pair, frame, rows, wid):
        @pl.when(s > 0)
        def _():
            pair[0].wait_recv()
            pair[1].wait_send()

        @pl.when(s < n - 1)
        def _():
            pair[1].wait_recv()
            pair[0].wait_send()

        zero = jnp.zeros((wid, frame.shape[1]), BF16)

        @pl.when(s == 0)
        def _():
            frame[pl.ds(0, wid), :] = zero

        @pl.when(s == n - 1)
        def _():
            frame[pl.ds((rows + 1) * wid, wid), :] = zero

    def merge(level):
        if level == 5:
            for copy in biases:
                copy.wait()
            if halved:
                partial.wait_recv()
                sums = own5[...] + in5[...]
            else:
                settle(L5)
                load5[0].wait()
                sums = jnp.dot(v5[0], w_l5[...], preferred_element_type=F32)
            m5[pl.ds(here, rows5 * wid5), :] = (sums + lb5[...]).astype(BF16)
            for j in range(1, n // 2):
                line_copy(j, s).start()
            pair_copy(0, s).start()
        elif level == 4:
            settle(L4)
            features[0].wait()
            for r in range(rows5):
                up = spread(m5[pl.ds(pl.multiple_of(here + r * wid5, 16), wid5), :])
                base = 2 * r * wid4
                lat = jnp.dot(v4[base : base + 2 * wid4, :], w_l4[...], preferred_element_type=F32)
                m4[wid4 + base : wid4 + base + 2 * wid4, :] = (
                    lat + lb4[...] + jnp.concatenate([up, up], axis=0)
                ).astype(BF16)
            start_halo(halos[0])
        else:
            settle(L3)
            features[1].wait()

            def coarse_row(r, carry):
                up = spread(m4[pl.ds(pl.multiple_of(wid4 + r * wid4, 16), wid4), :])
                base = pl.multiple_of(2 * r * wid3, 16)
                lat = jnp.dot(v3[pl.ds(base, 2 * wid3), :], w_l3[...], preferred_element_type=F32)
                m3[pl.ds(pl.multiple_of(wid3 + base, 16), 2 * wid3), :] = (
                    lat + lb3[...] + jnp.concatenate([up, up], axis=0)
                ).astype(BF16)
                return carry

            lax.fori_loop(0, rows4, coarse_row, 0)
            start_halo(halos[1])

    def smooth(level):
        if level == 3:
            settle(O3)
            end_halo(halos[1], m3, rows3, wid3)
            conv(m3, w_o3, ob3, r3, rows3, wid3, 4)
            return
        settle(O5)
        for j in range(n // 2):
            pair_copy(j, (across + n - 2 * j) % n).wait_recv()
        conv(m5, w_o5, ob5, r5, n * rows5, wid5, 16)
        few, many = r6.shape[0], r5.shape[0]
        pixel = lax.broadcasted_iota(jnp.int32, (few, many), 0)
        take = 2 * wid5 * (pixel // (wid5 // 2)) + 2 * (pixel % (wid5 // 2))
        pick = (take == lax.broadcasted_iota(jnp.int32, (few, many), 1)).astype(BF16)
        r6[...] = jnp.dot(pick, r5[...], preferred_element_type=F32).astype(BF16)

    def handle(kind, a, k, step):
        if kind == "push":
            push(a)
        elif kind == "pull":
            pull(a, k, step)
        elif kind == "mate":
            accept(a, k, step)
        elif kind == "swap":
            for copy in load5:
                copy.wait()
            swap.start()
        elif kind == "half":
            half_five()
        elif kind == "line":
            line_pull(a)
        elif kind == "merge":
            merge(a)
        else:
            smooth(a)

    for event in schedule(hops, lent, halved, n // 2):
        with jax.named_scope("_".join(map(str, event))):
            handle(*event)

    with jax.named_scope("last"):
        settle(O4)
        end_halo(halos[0], m4, rows4, wid4)
    for a in range(6):
        spot = bulk(a, parts[a] - lent[a], core)
        remote(spot, spot, ring_send.at[a], core_recv.at[a], partner).wait_send()
        if lent[a]:
            spot = bulk(a, lent[a], core)
            remote(spot, spot, mate_send.at[a], core_recv.at[a], partner).wait_send()
        spot = bulk(a, parts[a], core)
        remote(spot, spot, core_send.at[a], core_recv.at[a], partner).wait_send()
    for j in range(1, n // 2):
        line_copy(j, s).wait_send()
    for j in range(n // 2):
        pair_copy(j, s).wait_send()
    if halved:
        swap.wait_send()
        partial.wait_send()


def finish(dims, r3, r5, r6, m4, w_o4, ob4, y3, y4, y5, y6, r4, sems):
    (_, _), (rows4, wid4), _ = dims
    copies = [
        pltpu.make_async_copy(src, dst, sems.at[k])
        for k, (src, dst) in enumerate(((r3, y3), (r5, y5), (r6, y6)))
    ]
    for copy in copies:
        copy.start()
    conv(m4, w_o4, ob4, r4, rows4, wid4, rows4)
    copies.append(pltpu.make_async_copy(r4, y4, sems.at[3]))
    copies[3].start()
    for copy in copies:
        copy.wait()


def on_device(n, dps, *arrays):
    s3, s4, s5, l3, l4, l5, lb3, lb4, lb5, o3, o4, o5, ob3, ob4, ob5 = arrays
    dims = tuple(x.shape[1:3] for x in (s3, s4, s5))
    fd = l3.shape[1]
    (rows3, wid3), (rows4, wid4), (rows5, wid5) = dims
    flat = [x.reshape(-1, x.shape[3]) for x in (s3, s4, s5)]
    biases = [b.reshape(1, fd) for b in (lb3, lb4, lb5, ob3, ob4, ob5)]
    anywhere = pl.BlockSpec(memory_space=pl.ANY)
    near = pl.BlockSpec(memory_space=pltpu.VMEM)
    far = max(n // 2, 1)
    size5, wide5 = flat[2].shape
    deep5 = l5.shape[0]
    halved = dps % 4 == 0 and deep5 % 256 == 0
    split5 = 2 if halved else 1

    def array(*shape):
        return pltpu.VMEM(shape, BF16)

    def result(pixels):
        return jax.ShapeDtypeStruct((pixels, fd), BF16)

    dma = pltpu.SemaphoreType.DMA
    held = pl.pallas_call(
        functools.partial(kernel, n, dims, dps),
        out_shape=(
            array(rows3 * wid3, fd),
            array(n * rows5 * wid5, fd),
            array(n * rows5 * wid5 // 4, fd),
            array((rows4 + 2) * wid4, fd),
            array(3, 3, n * o4.shape[2], fd),
            pltpu.VMEM((1, fd), F32),
        ),
        in_specs=[anywhere] * 15,
        out_specs=(near,) * 6,
        scratch_shapes=[
            *(array(*x.shape) for x in flat[:2]),
            array(split5, size5, wide5 // split5),
            array(size5, wide5 // split5),
            *(pltpu.VMEM((size5, fd), F32) for _ in range(3)),
            array(n * deep5 // split5, fd),
            array(n * l4.shape[0], fd),
            array(n * l3.shape[0], fd),
            *(array(3, 3, n * x.shape[2], fd) for x in (o3, o5)),
            array((rows3 + 2) * wid3, fd),
            array((n * rows5 + 2) * wid5, fd),
            *(pltpu.VMEM((1, fd), F32) for _ in range(5)),
            dma((6,)),
            dma((6, 2, far)),
            dma((6,)),
            dma((6, 2, far)),
            dma((6,)),
            dma((6,)),
            dma((far,)),
            dma((far,)),
            dma((far,)),
            dma((far,)),
            dma((2,)),
            dma((2,)),
            dma((4,)),
            dma((4,)),
            dma((2,)),
            dma((14,)),
        ],
        compiler_params=pltpu.CompilerParams(
            collective_id=0, has_side_effects=True, vmem_limit_bytes=40 * 1024 * 1024
        ),
    )(*[
        pltpu.with_memory_space_constraint(x, pltpu.HBM)
        for x in (*flat, l3, l4, l5, *biases[:3], o3, o4, o5, *biases[3:])
    ])
    y3, y4, y5, y6 = pl.pallas_call(
        functools.partial(finish, dims),
        out_shape=(
            result(rows3 * wid3),
            result(rows4 * wid4),
            result(n * rows5 * wid5),
            result(n * rows5 * wid5 // 4),
        ),
        in_specs=[near] * 6,
        out_specs=(anywhere,) * 4,
        scratch_shapes=[array(rows4 * wid4, fd), dma((4,))],
        compiler_params=pltpu.CompilerParams(vmem_limit_bytes=32 * 1024 * 1024),
    )(*[pltpu.with_memory_space_constraint(x, pltpu.VMEM) for x in held])
    return (
        y3.reshape(1, rows3, wid3, fd),
        y4.reshape(1, rows4, wid4, fd),
        y5.reshape(1, n * rows5, wid5, fd),
        y6.reshape(1, n * rows5 // 2, wid5 // 2, fd),
    )


def solution(mesh):
    split, rows = P("dp", "space", None, None), P("space", None)
    taps = P(None, None, "space", None)
    whole = P("dp", None, None, None)
    return jax.shard_map(
        functools.partial(on_device, mesh.shape["space"], mesh.shape["dp"]),
        mesh=mesh,
        in_specs=(split,) * 3 + (rows,) * 3 + (P(),) * 3 + (taps,) * 3 + (P(),) * 3,
        out_specs=(split, split, whole, whole),
        check_vma=False,
    )
```

time: 52.3 us -> 38.2 us (0.73)
  the two profiles are of different devices: /device:TPU:15 before, /device:TPU:0 now
where the time goes in v1:
time: 38.2 us; the launch traced here: 38 us
  Pallas kernels  37.4 us (98%)
  between operations  0.65 us (2%)
    pallas_call x1, Pallas kernels, on_device(): pl.pallas_call(functools.partial(kernel, n, dims, dps), out_shape=(array(...  36.2 us
    pallas_call x1, Pallas kernels, on_device(): pl.pallas_call(functools.partial(finish, dims), out_shape=(result(rows3 *...  1.18 us

profile of v1, /device:TPU:0, one launch (start us, length us, event | category | flops | bytes accessed | tf_op | source)
XLA Modules:
  0.0 38.0 jit_solution(8147975793415500616)
XLA Ops:
  0.6 36.2 %shard_map.174 = (bf16[1024,256]{1,0:T(8,128)(2,1)S(1)}, bf16[512,256]{1,0:T(8,128)(2,1)S(1)}, bf16[128,256]{1,0:T(8,128)(2,1)S(1)}, bf16[384,256]{1,0:T(8,128)(...) custom-call(bf16[1024,512]{1,0:T(8,128)(2,1)} %bitcast.13, bf16[256,1024]{1,0:T(8,128)(2,1)} %bitcast.14, ...), custom_call_target="tpu_custom_call" | custom-call | tf_op jit(solution)/shard_map/pallas_call | solution.py:459
  36.8 1.2 %shard_map.175 = (bf16[1024,256]{1,0:T(8,128)(2,1)}, bf16[256,256]{1,0:T(8,128)(2,1)}, bf16[512,256]{1,0:T(8,128)(2,1)}, bf16[128,256]{1,0:T(8,128)(2,1)}) custom-call(bf16[1024,256]{1,0:T(8,128)(2,1)S(1)} %get-tuple-element.14.r3, bf16[512,256]{1,0:T(8,128)(2,1)S(1)} %get-tuple-element.15.r5, bf16[128,256]{1,0:T(8,128)(2,1)S(1)} %get-tuple-element.16.r6, ...), custom_call_target="tpu_custom_call" | custom-call | tf_op jit(solution)/shard_map/pallas_call | solution.py:507

commit v2 on v1

v2 whole, which is shorter than its diff:
```python
import functools

import jax
import jax.numpy as jnp
from jax import lax
from jax.experimental import pallas as pl
from jax.experimental.pallas import tpu as pltpu
from jax.sharding import PartitionSpec as P

F32, BF16 = jnp.float32, jnp.bfloat16
L5, L4, L3, O3, O5, O4 = range(6)


def ring_place(s, n):
    return s // 2 + (s % 2) * (n - 1 - 2 * (s // 2))


def ring_owner(place, n):
    r = (place + 2 * n) % n
    back = r // (n // 2)
    return (1 - back) * (2 * r) + back * (2 * (n - 1 - r) + 1)


def spread(coarse):
    pixels = coarse.shape[0]
    fine = lax.broadcasted_iota(jnp.int32, (2 * pixels, pixels), 0) // 2
    pick = (fine == lax.broadcasted_iota(jnp.int32, (2 * pixels, pixels), 1)).astype(BF16)
    return jnp.dot(pick, coarse, preferred_element_type=F32)


def conv_tile(frame, weight, bias, start, pixels, width):
    rows = jnp.concatenate(
        [frame[pl.ds(pl.multiple_of(start + a * width, 16), pixels), :] for a in range(3)], axis=1
    )
    depth = weight.shape[2]
    part = [
        jnp.dot(
            rows,
            weight[:, c].reshape(3 * depth, weight.shape[3]),
            preferred_element_type=F32,
        )
        for c in range(3)
    ]
    column = lax.broadcasted_iota(jnp.int32, (pixels, 1), 0) % width
    left = jnp.where(column == 0, 0.0, pltpu.roll(part[0], 1, 0))
    right = jnp.where(column == width - 1, 0.0, pltpu.roll(part[2], pixels - 1, 0))
    return part[1] + left + right + bias[...]


def conv(frame, weight, bias, out, rows, wid, tall, first=0):
    def tile(i, carry):
        start = pl.multiple_of(i * (tall * wid), 16)
        out[pl.ds(start, tall * wid), :] = conv_tile(
            frame, weight, bias, start, tall * wid, wid
        ).astype(BF16)
        return carry

    lax.fori_loop(first, rows // tall, tile, 0)


def shared(unit, parts, split):
    if not split:
        return 0
    return parts // 2 // unit * unit if unit > 1 else parts // 3


PUSH, PULL, MATE, SWAP, HALF, PRE, MERGE, REST, LINE, CONV = range(10)
ORDER = (
    100, 0, 500, 400, 1111, 3000, 200, 1101, 1011, 1001, 1501, 300, 1102, 1411, 1201, 1112,
    1012, 1002, 1511, 1401, 1211, 1301, 1412, 1103, 1003, 1202, 1113, 1502, 2102, 1013, 1402,
    1302, 1212, 2401, 1104, 1311, 1004, 4000, 1203, 1303, 1512, 2103, 2104, 2101, 1503, 1312,
    1213, 1403, 5400, 1204, 6500, 6400, 5300, 1313, 1304, 1413, 2502, 6300, 1513, 1404, 2402,
    2303, 2301, 1504, 8200, 2302, 2304, 8300, 2501, 8100, 7300, 2503, 2403, 2404, 9300, 2504,
    9500,
)
ROWS = (O4,)
WHOLE = (L3,)


def schedule(hops, lent, halved, line):
    begin = (2.34, 0.36, 2.39, 5.66, 3.55, 2.90)
    pace = (2.10, 2.62, 2.56, 3.93, 4.11, 5.31)
    lag = (2.50, 4.29, 5.09, 6.74, 3.76, 6.04)
    settled, half_to_five, line_lag, three_to_conv = 1.21, 4.39, 6.36, 3.0
    timed = [(0.5, (SWAP, 0, 0, 0))]
    ready = []
    for a in range(6):
        timed.append((begin[a], (PUSH, a, 0, 0)))
        for k in range(2):
            for step in range(1, hops[k] + 1):
                at = begin[a] + pace[a] * step
                timed.append((at, (PULL, a, k, step)))
                if lent[a] and k == 0:
                    timed.append((at + lag[a], (MATE, a, 0, step)))
        ready.append(begin[a] + pace[a] * hops[0] + (lag[a] if lent[a] else 0.0) + 0.001)
    five = ready[L5] + settled
    if halved:
        timed.append((five, (HALF, 0, 0, 0)))
        five += half_to_five
    four = max(five, ready[L4] + settled) + 0.01
    three = max(four, ready[L3] + settled) + 0.01
    conv = max(three + three_to_conv, ready[O3])
    timed += [
        (ready[L4] + settled, (PRE, 4, 0, 0)),
        (ready[L3] + settled, (PRE, 3, 0, 0)),
        (five, (MERGE, 5, 0, 0)),
        (four, (MERGE, 4, 0, 0)),
        (three, (MERGE, 3, 0, 0)),
        (three + 0.001, (REST, 3, 0, 0)),
        (conv, (CONV, 3, 0, 0)),
        (max(conv, five + line_lag, ready[O5]) + 0.5, (CONV, 5, 0, 0)),
    ]
    timed += [(five + line_lag + 0.01 * j, (LINE, j, 0, 0)) for j in range(1, line)]
    events = [e for _, e in sorted(timed, key=lambda e: e[0])]
    tuned = [(c // 1000, c // 100 % 10, c // 10 % 10, c % 10) for c in ORDER]
    return tuned if sorted(tuned) == sorted(events) else events


def kernel(
    n, dims, dps,
    s3, s4, s5, l3, l4, l5, hb3, hb4, hb5, o3, o4, o5, hc3, hc4, hc5,
    r3, r4, r5, r6,
    v3, v4, v5, v5_mate, own5, out5, in5, w_l5, w_l4, w_l3, w_o3, w_o5, w_o4,
    m3, m4, m5, part3, part4, bias,
    sent, ring_recv, mate_recv, core_recv, map_sent, line_recv, pair_recv,
    swap_sent, partial_sent, swap_recv, halo_send, halo_recv, local_sem,
):
    (rows3, wid3), (rows4, wid4), (rows5, wid5) = dims
    dp, s = lax.axis_index("dp"), lax.axis_index("space")
    core = dp % 2
    plane = (dp // 2) % 2
    partner = (dp + 1 - 2 * core, s)
    mate = (dp + 2 - 4 * plane, s)
    paired = dps % 4 == 0
    place = ring_place(s, n)
    sign = 1 - 2 * core
    hops = (n // 2, n - 1 - n // 2)
    turn = (sign, -sign)
    target = [(dp, ring_owner(place + turn[k], n)) for k in range(2)]
    above, below = (dp, (s + n - 1) % n), (dp, (s + 1) % n)

    full = (w_l5, w_l4, w_l3, w_o3, w_o5, w_o4)
    mine = (l5, l4, l3, o3, o5, o4)
    half = w_l5.shape[1] // 2

    barrier = pltpu.get_barrier_semaphore()
    friends = [*target, partner] + ([mate] if paired else [])
    for device in friends:
        pl.semaphore_signal(
            barrier, inc=1, device_id=device, device_id_type=pl.DeviceIdType.MESH
        )

    size = o3.shape[2]
    by_rows = [False] * 3 + [size % 32 == 0 and a in ROWS for a in range(3, 6)]
    parts = [mine[a].shape[0] for a in range(3)] + [size if by_rows[a] else 3 for a in range(3, 6)]
    lent = [
        shared(16 if a < 3 or by_rows[a] else 1, parts[a], paired and a not in WHOLE) for a in range(6)
    ]
    halved = v5.shape[0] == 2
    if halved:
        parts[L5], lent[L5] = parts[L5] // 2, 0

    def chunk(a, owner, side, first, count):
        cols = pl.ds(pl.multiple_of(side * half, half), half)
        if a < 3:
            return full[a].at[pl.ds(pl.multiple_of(owner * parts[a] + first, 16), count), cols]
        if by_rows[a]:
            return full[a].at[
                :, :, pl.ds(pl.multiple_of(owner * size + first, 16), count), cols
            ]
        return full[a].at[
            pl.ds(first, count), :, pl.ds(pl.multiple_of(owner * size, size), size), cols
        ]

    def ring_part(a, owner):
        return chunk(a, owner, core, plane * lent[a], parts[a] - lent[a])

    def mate_part(a, owner, sender):
        return chunk(a, owner, core, sender * (parts[a] - lent[a]), lent[a])

    def own_whole(a):
        if a < 3:
            return full[a].at[pl.ds(pl.multiple_of(s * parts[a], parts[a]), parts[a]), :]
        return full[a].at[:, :, pl.ds(pl.multiple_of(s * size, size), size), :]

    def own_shard(a):
        if a == L5 and halved:
            return mine[a].at[pl.ds(pl.multiple_of(plane * parts[a], 16), parts[a]), :]
        return mine[a]

    def bulk(a, count, owners, cols):
        if a < 3:
            return full[a].at[pl.ds(0, owners * count), cols]
        if by_rows[a]:
            return full[a].at[:, :, pl.ds(0, owners * count), cols]
        return full[a].at[pl.ds(0, count), :, pl.ds(0, owners * size), cols]

    one_side, both_sides = pl.ds(0, half), pl.ds(0, 2 * half)

    local = [pltpu.make_async_copy(own_shard(a), own_whole(a), local_sem.at[a]) for a in range(6)]
    features = [
        pltpu.make_async_copy(src, dst, local_sem.at[6 + k])
        for k, (src, dst) in enumerate(((s4, v4), (s3, v3)))
    ]
    bias_rows = [
        pltpu.make_async_copy(src, bias.at[pl.ds(k, 1), :], local_sem.at[8 + k])
        for k, src in enumerate((hb3, hb4, hb5, hc3, hc4, hc5))
    ]
    load5 = [
        pltpu.make_async_copy(s5.at[:, pl.ds(0, v5.shape[2])], v5.at[q], local_sem.at[14 + q])
        for q in range(v5.shape[0])
    ]
    lb3, lb4, lb5, ob3, ob4, ob5 = (bias.at[pl.ds(k, 1), :] for k in range(6))
    for copy in local:
        copy.start()
    if halved:
        for q in range(2):
            for owner in range(n):
                pltpu.make_async_copy(
                    s5.at[:, pl.ds((2 * owner + q) * parts[L5], parts[L5])],
                    v5.at[q, :, pl.ds(owner * parts[L5], parts[L5])],
                    local_sem.at[14 + q],
                ).start()
    else:
        load5[0].start()
    for copy in features + bias_rows:
        copy.start()

    zero5 = jnp.zeros((wid5, m5.shape[1]), BF16)
    m5[pl.ds(0, wid5), :] = zero5
    m5[pl.ds(m5.shape[0] - wid5, wid5), :] = zero5
    with jax.named_scope("meet"):
        pl.semaphore_wait(barrier, len(friends))

    def remote(src, dst, send, recv, device):
        return pltpu.make_async_remote_copy(
            src_ref=src, dst_ref=dst, send_sem=send, recv_sem=recv,
            device_id=device, device_id_type=pl.DeviceIdType.MESH,
        )

    def send(a, k, step, owner):
        if step <= hops[k]:
            spot = ring_part(a, owner)
            remote(spot, spot, sent.at[a], ring_recv.at[a, k * hops[0] + step - 1], target[k]).start()

    def cross(a, spot):
        remote(spot, spot, sent.at[a], core_recv.at[a], partner).start()

    def push(a):
        local[a].wait()
        for k in range(2):
            send(a, k, 1, s)

    def pull(a, k, step):
        owner = ring_owner(place - turn[k] * step, n)
        spot = ring_part(a, owner)
        sem = ring_recv.at[a, k * hops[0] + step - 1]
        remote(spot, spot, sent.at[a], sem, target[k]).wait_recv()
        send(a, k, step + 1, owner)
        if lent[a]:
            gift = mate_part(a, owner, plane)
            remote(gift, gift, sent.at[a], mate_recv.at[a, step - 1], mate).start()
        cross(a, spot)

    def accept(a, step):
        both = [k for k in range(2) if step <= hops[k]]
        spot = bulk(a, lent[a], len(both), one_side)
        remote(spot, spot, sent.at[a], mate_recv.at[a, step - 1], mate).wait_recv()
        for k in both:
            owner = ring_owner(place - turn[k] * step, n)
            cross(a, mate_part(a, owner, 1 - plane))

    def settle(a):
        spot = bulk(a, parts[a], n - 1, one_side)
        remote(spot, spot, sent.at[a], core_recv.at[a], partner).wait_recv()

    def drain(arrays):
        for a in arrays:
            spot = bulk(a, parts[a], n - 1, both_sides)
            remote(spot, spot, sent.at[a], core_recv.at[a], partner).wait_send()

    def map_rows(owner):
        count = rows5 * wid5
        return m5.at[pl.ds(pl.multiple_of(wid5 + owner * count, 16), count), :]

    across = s + 1 - 2 * (s % 2)

    def line_copy(j, owner):
        spot = map_rows(owner)
        peer = (dp, (s + 2 * j) % n)
        return remote(spot, spot, map_sent, line_recv.at[j - 1], peer)

    def pair_copy(owner):
        spot = map_rows(owner)
        return remote(spot, spot, map_sent, pair_recv, (dp, across))

    def map_view(count):
        return m5.at[pl.ds(0, count * rows5 * wid5), :]

    def line_pull(j):
        owner = (s + n - 2 * j) % n
        line_copy(j, owner).wait_recv()
        pair_copy(owner).start()

    if halved:
        swap = remote(v5.at[1 - plane], v5_mate, swap_sent, swap_recv.at[0], mate)
        partial = remote(out5, in5, partial_sent, swap_recv.at[1], mate)

    def half_five():
        settle(L5)
        swap.wait_recv()
        rows = jnp.concatenate([v5[plane], v5_mate[...]], axis=0)
        sums = jnp.dot(rows, w_l5[...], preferred_element_type=F32)
        own5[...] = sums[: own5.shape[0]]
        out5[...] = sums[own5.shape[0] :]
        partial.start()

    here = pl.multiple_of(wid5 + s * (rows5 * wid5), 16)
    halos = []
    for k, (frame, rows, wid) in enumerate(((m4, rows4, wid4), (m3, rows3, wid3))):
        first, last = frame.at[pl.ds(wid, wid), :], frame.at[pl.ds(rows * wid, wid), :]
        top, bottom = frame.at[pl.ds(0, wid), :], frame.at[pl.ds((rows + 1) * wid, wid), :]
        halos.append((
            remote(last, top, halo_send.at[2 * k], halo_recv.at[2 * k], below),
            remote(first, bottom, halo_send.at[2 * k + 1], halo_recv.at[2 * k + 1], above),
        ))

    def start_halo(pair):
        @pl.when(s < n - 1)
        def _():
            pair[0].start()

        @pl.when(s > 0)
        def _():
            pair[1].start()

    def end_halo(pair, frame, rows, wid):
        @pl.when(s > 0)
        def _():
            pair[0].wait_recv()
            pair[1].wait_send()

        @pl.when(s < n - 1)
        def _():
            pair[1].wait_recv()
            pair[0].wait_send()

        zero = jnp.zeros((wid, frame.shape[1]), BF16)

        @pl.when(s == 0)
        def _():
            frame[pl.ds(0, wid), :] = zero

        @pl.when(s == n - 1)
        def _():
            frame[pl.ds((rows + 1) * wid, wid), :] = zero

    def prepare(level):
        if level == 4:
            settle(L4)
            features[0].wait()
            part4[...] = jnp.dot(v4[...], w_l4[...], preferred_element_type=F32) + lb4[...]
            return
        settle(L3)
        features[1].wait()
        tall = 2 * wid3

        def tile(i, carry):
            span = pl.ds(pl.multiple_of(i * tall, tall), tall)
            part3[span, :] = (
                jnp.dot(v3[span, :], w_l3[...], preferred_element_type=F32) + lb3[...]
            )
            return carry

        lax.fori_loop(0, rows4, tile, 0)

    def add_row(r, coarse, fine, part, wid):
        up = spread(coarse[pl.ds(pl.multiple_of(wid + r * wid, 16), wid), :])
        base = pl.multiple_of(4 * r * wid, 16)
        fine[pl.ds(pl.multiple_of(2 * wid + base, 16), 4 * wid), :] = (
            part[pl.ds(base, 4 * wid), :] + jnp.concatenate([up, up], axis=0)
        ).astype(BF16)

    def merge(level):
        if level == 5:
            if halved:
                partial.wait_recv()
                sums = own5[...] + in5[...]
            else:
                settle(L5)
                sums = jnp.dot(v5[0], w_l5[...], preferred_element_type=F32)
            m5[pl.ds(here, rows5 * wid5), :] = (sums + lb5[...]).astype(BF16)
            for j in range(1, n // 2):
                line_copy(j, s).start()
            pair_copy(s).start()
        elif level == 4:
            own_five = m5.at[pl.ds(pl.multiple_of(here - wid5, 16), (rows5 + 1) * wid5), :]
            for r in range(rows5):
                add_row(r, own_five, m4, part4, wid5)
            start_halo(halos[0])
        else:
            for r in sorted({0, rows4 - 1}):
                add_row(r, m4, m3, part3, wid4)
            start_halo(halos[1])

    def rest():
        def row(r, carry):
            add_row(r, m4, m3, part3, wid4)
            return carry

        lax.fori_loop(1, rows4 - 1, row, 0)

    def smooth(level):
        if level == 3:
            settle(O3)
            end_halo(halos[1], m3, rows3, wid3)
            conv(m3, w_o3, ob3, r3, rows3, wid3, 4)
            return
        if level == 4:
            settle(O4)
            end_halo(halos[0], m4, rows4, wid4)
            conv(m4, w_o4, ob4, r4, rows4, wid4, rows4)
            return
        settle(O5)
        spot = map_view(n // 2)
        remote(spot, spot, map_sent, pair_recv, (dp, across)).wait_recv()
        conv(m5, w_o5, ob5, r5, n * rows5, wid5, 16)
        few, many = r6.shape[0], r5.shape[0]
        pixel = lax.broadcasted_iota(jnp.int32, (few, many), 0)
        take = 2 * wid5 * (pixel // (wid5 // 2)) + 2 * (pixel % (wid5 // 2))
        pick = (take == lax.broadcasted_iota(jnp.int32, (few, many), 1)).astype(BF16)
        r6[...] = jnp.dot(pick, r5[...], preferred_element_type=F32).astype(BF16)

    def start_swap():
        for copy in load5 + bias_rows:
            copy.wait()
        if halved:
            swap.start()

    def handle(kind, a, k, step):
        if kind == PUSH:
            push(a)
        elif kind == PULL:
            pull(a, k, step)
        elif kind == MATE:
            accept(a, step)
        elif kind == SWAP:
            start_swap()
        elif kind == HALF:
            half_five()
        elif kind == PRE:
            prepare(a)
        elif kind == MERGE:
            merge(a)
        elif kind == REST:
            rest()
        elif kind == LINE:
            line_pull(a)
        else:
            smooth(a)

    def drain_maps():
        spot = map_view(n - 1)
        remote(spot, spot, map_sent, pair_recv, (dp, across)).wait_send()
        if halved:
            swap.wait_send()
            partial.wait_send()

    for event in schedule(hops, lent, halved, n // 2):
        if event[:2] == (CONV, 5):
            drain((L5, L4, L3))
        with jax.named_scope("_".join(map(str, event))):
            handle(*event)

    with jax.named_scope("drain_maps"):
        drain_maps()
    with jax.named_scope("last"):
        smooth(4)
    with jax.named_scope("drain"):
        drain((O3, O5, O4))


def finish(*refs):
    results, outputs, sems = refs[:4], refs[4:8], refs[8]
    copies = [
        pltpu.make_async_copy(src, dst, sems.at[k])
        for k, (src, dst) in enumerate(zip(results, outputs))
    ]
    for copy in copies:
        copy.start()
    for copy in copies:
        copy.wait()


def on_device(n, dps, *arrays):
    s3, s4, s5, l3, l4, l5, lb3, lb4, lb5, o3, o4, o5, ob3, ob4, ob5 = arrays
    dims = tuple(x.shape[1:3] for x in (s3, s4, s5))
    fd = l3.shape[1]
    (rows3, wid3), (rows4, wid4), (rows5, wid5) = dims
    flat = [x.reshape(-1, x.shape[3]) for x in (s3, s4, s5)]
    biases = [b.reshape(1, fd) for b in (lb3, lb4, lb5, ob3, ob4, ob5)]
    anywhere = pl.BlockSpec(memory_space=pl.ANY)
    near = pl.BlockSpec(memory_space=pltpu.VMEM)
    far = max(n // 2, 1)
    size5, wide5 = flat[2].shape
    deep5 = l5.shape[0]
    halved = dps % 4 == 0 and deep5 % 256 == 0
    split5 = 2 if halved else 1

    def array(*shape):
        return pltpu.VMEM(shape, BF16)

    def result(pixels):
        return jax.ShapeDtypeStruct((pixels, fd), BF16)

    dma = pltpu.SemaphoreType.DMA
    held = pl.pallas_call(
        functools.partial(kernel, n, dims, dps),
        out_shape=(
            array(rows3 * wid3, fd),
            array(rows4 * wid4, fd),
            array(n * rows5 * wid5, fd),
            array(n * rows5 * wid5 // 4, fd),
        ),
        in_specs=[anywhere] * 15,
        out_specs=(near,) * 4,
        scratch_shapes=[
            *(array(*x.shape) for x in flat[:2]),
            array(split5, size5, wide5 // split5),
            array(size5, wide5 // split5),
            *(pltpu.VMEM((size5, fd), F32) for _ in range(3)),
            array(n * deep5 // split5, fd),
            array(n * l4.shape[0], fd),
            array(n * l3.shape[0], fd),
            *(array(3, 3, n * x.shape[2], fd) for x in (o3, o5, o4)),
            array((rows3 + 2) * wid3, fd),
            array((rows4 + 2) * wid4, fd),
            array((n * rows5 + 2) * wid5, fd),
            pltpu.VMEM((rows3 * wid3, fd), F32),
            pltpu.VMEM((rows4 * wid4, fd), F32),
            pltpu.VMEM((6, fd), F32),
            dma((6,)),
            dma((6, n - 1)),
            dma((6, far)),
            dma((6,)),
            dma,
            dma((far,)),
            dma,
            dma,
            dma,
            dma((2,)),
            dma((4,)),
            dma((4,)),
            dma((16,)),
        ],
        compiler_params=pltpu.CompilerParams(
            collective_id=0, has_side_effects=True, vmem_limit_bytes=40 * 1024 * 1024
        ),
    )(*[
        pltpu.with_memory_space_constraint(x, pltpu.HBM)
        for x in (*flat, l3, l4, l5, *biases[:3], o3, o4, o5, *biases[3:])
    ])
    y3, y4, y5, y6 = pl.pallas_call(
        finish,
        out_shape=(
            result(rows3 * wid3),
            result(rows4 * wid4),
            result(n * rows5 * wid5),
            result(n * rows5 * wid5 // 4),
        ),
        in_specs=[near] * 4,
        out_specs=(anywhere,) * 4,
        scratch_shapes=[dma((4,))],
        compiler_params=pltpu.CompilerParams(vmem_limit_bytes=32 * 1024 * 1024),
    )(*[pltpu.with_memory_space_constraint(x, pltpu.VMEM) for x in held])
    return (
        y3.reshape(1, rows3, wid3, fd),
        y4.reshape(1, rows4, wid4, fd),
        y5.reshape(1, n * rows5, wid5, fd),
        y6.reshape(1, n * rows5 // 2, wid5 // 2, fd),
    )


def solution(mesh):
    split, rows = P("dp", "space", None, None), P("space", None)
    taps = P(None, None, "space", None)
    whole = P("dp", None, None, None)
    return jax.shard_map(
        functools.partial(on_device, mesh.shape["space"], mesh.shape["dp"]),
        mesh=mesh,
        in_specs=(split,) * 3 + (rows,) * 3 + (P(),) * 3 + (taps,) * 3 + (P(),) * 3,
        out_specs=(split, split, whole, whole),
        check_vma=False,
    )
```

time: 38.2 us -> 35.3 us (0.924)
  Pallas kernels: 37.4 us -> 34.5 us
    pallas_call x1, Pallas kernels: 36.2 us -> 33.6 us  [on_device(): pl.pallas_call(functools.partial(kernel, n, dims, dps), out_shape=(array(...]
where the time goes in v2:
time: 35.3 us; the launch traced here: 35.2 us
  Pallas kernels  34.5 us (98%)
  between operations  0.65 us (2%)
    pallas_call x1, Pallas kernels, on_device(): pl.pallas_call(functools.partial(kernel, n, dims, dps), out_shape=(array(...  33.6 us
    pallas_call x1, Pallas kernels, on_device(): pl.pallas_call(finish, out_shape=(result(rows3 * wid3), result(rows4 * wi...  0.97 us

profile of v2, /device:TPU:0, one launch (start us, length us, event | category | flops | bytes accessed | tf_op | source)
XLA Modules:
  0.0 35.2 jit_solution(15812110866192431524)
XLA Ops:
  0.6 33.6 %shard_map.174 = (bf16[1024,256]{1,0:T(8,128)(2,1)S(1)}, bf16[256,256]{1,0:T(8,128)(2,1)S(1)}, bf16[512,256]{1,0:T(8,128)(2,1)S(1)}, bf16[128,256]{1,0:T(8,128)(2,1)S(1)}) custom-call(bf16[1024,512]{1,0:T(8,128)(2,1)} %bitcast.13, bf16[256,1024]{1,0:T(8,128)(2,1)} %bitcast.14, bf16[64,2048]{1,0:T(8,128)(2,1)} %bitcast.15, bf16[64,256]{1,0:T(8,128)(2,1)} %l3.1, ...), custom_call_target="tpu_custom_call" | custom-call | tf_op jit(solution)/shard_map/pallas_call | solution.py:517
  34.2 1.0 %shard_map.175 = (bf16[1024,256]{1,0:T(8,128)(2,1)}, bf16[256,256]{1,0:T(8,128)(2,1)}, bf16[512,256]{1,0:T(8,128)(2,1)}, bf16[128,256]{1,0:T(8,128)(2,1)}) custom-call(bf16[1024,256]{1,0:T(8,128)(2,1)S(1)} %get-tuple-element.12.refs_0_, bf16[256,256]{1,0:T(8,128)(2,1)S(1)} %get-tuple-element.13.refs_1_, bf16[512,256]{1,0:T(8,128)(2,1)S(1)} %get-tuple-element.14.refs_2_, ...), custom_call_target="tpu_custom_call" | custom-call | tf_op jit(solution)/shard_map/pallas_call | solution.py:563

commit v3 on v2

--- a/solution.py
+++ b/solution.py
@@ -66,11 +66,11 @@
 
 PUSH, PULL, MATE, SWAP, HALF, PRE, MERGE, REST, LINE, CONV = range(10)
 ORDER = (
-    100, 0, 500, 400, 1111, 3000, 200, 1101, 1011, 1001, 1501, 300, 1102, 1411, 1201, 1112,
-    1012, 1002, 1511, 1401, 1211, 1301, 1412, 1103, 1003, 1202, 1113, 1502, 2102, 1013, 1402,
-    1302, 1212, 2401, 1104, 1311, 1004, 4000, 1203, 1303, 1512, 2103, 2104, 2101, 1503, 1312,
-    1213, 1403, 5400, 1204, 6500, 6400, 5300, 1313, 1304, 1413, 2502, 6300, 1513, 1404, 2402,
-    2303, 2301, 1504, 8200, 2302, 2304, 8300, 2501, 8100, 7300, 2503, 2403, 2404, 9300, 2504,
+    100, 0, 200, 500, 300, 3000, 1101, 1001, 1201, 1011, 1111, 1511, 400, 1501, 1102, 1002,
+    1012, 1112, 1301, 1401, 1512, 1103, 1211, 2501, 2101, 1003, 1502, 1013, 1202, 1311, 1113,
+    2102, 1402, 1104, 1411, 1302, 1004, 1212, 4000, 1312, 1203, 1403, 1513, 1303, 2104, 2103,
+    1412, 1503, 5400, 6500, 1213, 1204, 6400, 5300, 1413, 1313, 2302, 6300, 1304, 1404, 8300,
+    2502, 8200, 8100, 2403, 2301, 2503, 1504, 2303, 2401, 2304, 7300, 2404, 2402, 9300, 2504,
     9500,
 )
 ROWS = (O4,)

time: 35.3 us -> 34.6 us (0.980)
  Pallas kernels: 34.5 us -> 33.8 us
    pallas_call x1, Pallas kernels: 33.6 us -> 32.8 us  [on_device(): pl.pallas_call(functools.partial(kernel, n, dims, dps), out_shape=(array(...]
where the time goes in v3:
time: 34.6 us; the launch traced here: 34.4 us
  Pallas kernels  33.8 us (98%)
  between operations  0.65 us (2%)
    pallas_call x1, Pallas kernels, on_device(): pl.pallas_call(functools.partial(kernel, n, dims, dps), out_shape=(array(...  32.8 us
    pallas_call x1, Pallas kernels, on_device(): pl.pallas_call(finish, out_shape=(result(rows3 * wid3), result(rows4 * wi...  0.97 us

profile of v3, /device:TPU:0, one launch (start us, length us, event | category | flops | bytes accessed | tf_op | source)
XLA Modules:
  0.0 34.4 jit_solution(9639765673004977015)
XLA Ops:
  0.6 32.8 %shard_map.174 = (bf16[1024,256]{1,0:T(8,128)(2,1)S(1)}, bf16[256,256]{1,0:T(8,128)(2,1)S(1)}, bf16[512,256]{1,0:T(8,128)(2,1)S(1)}, bf16[128,256]{1,0:T(8,128)(2,1)S(1)}) custom-call(bf16[1024,512]{1,0:T(8,128)(2,1)} %bitcast.13, bf16[256,1024]{1,0:T(8,128)(2,1)} %bitcast.14, bf16[64,2048]{1,0:T(8,128)(2,1)} %bitcast.15, bf16[64,256]{1,0:T(8,128)(2,1)} %l3.1, ...), custom_call_target="tpu_custom_call" | custom-call | tf_op jit(solution)/shard_map/pallas_call | solution.py:517
  33.5 1.0 %shard_map.175 = (bf16[1024,256]{1,0:T(8,128)(2,1)}, bf16[256,256]{1,0:T(8,128)(2,1)}, bf16[512,256]{1,0:T(8,128)(2,1)}, bf16[128,256]{1,0:T(8,128)(2,1)}) custom-call(bf16[1024,256]{1,0:T(8,128)(2,1)S(1)} %get-tuple-element.12.refs_0_, bf16[256,256]{1,0:T(8,128)(2,1)S(1)} %get-tuple-element.13.refs_1_, bf16[512,256]{1,0:T(8,128)(2,1)S(1)} %get-tuple-element.14.refs_2_, ...), custom_call_target="tpu_custom_call" | custom-call | tf_op jit(solution)/shard_map/pallas_call | solution.py:563

commit v4 on v3

--- a/solution.py
+++ b/solution.py
@@ -312,7 +312,7 @@
         rows = jnp.concatenate([v5[plane], v5_mate[...]], axis=0)
         sums = jnp.dot(rows, w_l5[...], preferred_element_type=F32)
         own5[...] = sums[: own5.shape[0]]
-        out5[...] = sums[own5.shape[0] :]
+        out5[...] = sums[own5.shape[0] :].astype(BF16)
         partial.start()
 
     here = pl.multiple_of(wid5 + s * (rows5 * wid5), 16)
@@ -385,7 +385,7 @@
         if level == 5:
             if halved:
                 partial.wait_recv()
-                sums = own5[...] + in5[...]
+                sums = own5[...] + in5[...].astype(F32)
             else:
                 settle(L5)
                 sums = jnp.dot(v5[0], w_l5[...], preferred_element_type=F32)
@@ -528,7 +528,8 @@
             *(array(*x.shape) for x in flat[:2]),
             array(split5, size5, wide5 // split5),
             array(size5, wide5 // split5),
-            *(pltpu.VMEM((size5, fd), F32) for _ in range(3)),
+            pltpu.VMEM((size5, fd), F32),
+            *(array(size5, fd) for _ in range(2)),
             array(n * deep5 // split5, fd),
             array(n * l4.shape[0], fd),
             array(n * l3.shape[0], fd),

time: 34.6 us -> 34.3 us (level)
  no operation moved by 1% of the time
where the time goes in v4:
time: 34.3 us; the launch traced here: 34.2 us
  Pallas kernels  33.5 us (98%)
  between operations  0.65 us (2%)
    pallas_call x1, Pallas kernels, on_device(): pl.pallas_call(functools.partial(kernel, n, dims, dps), out_shape=(array(...  32.5 us
    pallas_call x1, Pallas kernels, on_device(): pl.pallas_call(finish, out_shape=(result(rows3 * wid3), result(rows4 * wi...  0.97 us

profile of v4, /device:TPU:0, one launch (start us, length us, event | category | flops | bytes accessed | tf_op | source)
XLA Modules:
  0.0 34.2 jit_solution(15564583716264860459)
XLA Ops:
  0.6 32.5 %shard_map.174 = (bf16[1024,256]{1,0:T(8,128)(2,1)S(1)}, bf16[256,256]{1,0:T(8,128)(2,1)S(1)}, bf16[512,256]{1,0:T(8,128)(2,1)S(1)}, bf16[128,256]{1,0:T(8,128)(2,1)S(1)}) custom-call(bf16[1024,512]{1,0:T(8,128)(2,1)} %bitcast.13, bf16[256,1024]{1,0:T(8,128)(2,1)} %bitcast.14, bf16[64,2048]{1,0:T(8,128)(2,1)} %bitcast.15, bf16[64,256]{1,0:T(8,128)(2,1)} %l3.1, ...), custom_call_target="tpu_custom_call" | custom-call | tf_op jit(solution)/shard_map/pallas_call | solution.py:517
  33.2 1.0 %shard_map.175 = (bf16[1024,256]{1,0:T(8,128)(2,1)}, bf16[256,256]{1,0:T(8,128)(2,1)}, bf16[512,256]{1,0:T(8,128)(2,1)}, bf16[128,256]{1,0:T(8,128)(2,1)}) custom-call(bf16[1024,256]{1,0:T(8,128)(2,1)S(1)} %get-tuple-element.12.refs_0_, bf16[256,256]{1,0:T(8,128)(2,1)S(1)} %get-tuple-element.13.refs_1_, bf16[512,256]{1,0:T(8,128)(2,1)S(1)} %get-tuple-element.14.refs_2_, ...), custom_call_target="tpu_custom_call" | custom-call | tf_op jit(solution)/shard_map/pallas_call | solution.py:564
